TPU v7x, 32 devices: a whole 2x2x4 slice. The times are simulated.
32 devices in a mesh: dom: 8 (over y, x, core), grp: 4 (over z).
Axes of the slice: x: 2, y: 2, z: 4, core: 2. Of those that a mesh axis runs over, the one named last changes fastest.
Arguments:
- solved: bfloat16 [8, 4096, 512], P('dom', 'grp'), may hold values from -6 to 6
- e_blocks: bfloat16 [8, 6, 4096, 1024], P('dom', None, 'grp'), may hold values from -0.125 to 0.125
- block_mask: int32 [8, 6, 4], P('dom', None, 'grp'), may hold values 0 or 1
- owner: int32 [8, 6, 1], P('dom'), may hold values from 0 to 7; in each aligned block of 6 rows (0 to 5, 6 to 11, ..., all dimensions but the last counted through in order) at most 2 rows name the same one
- local_id: int32 [8, 6], P('dom'), may hold values from 0 to 3
Outputs:
- schur: bfloat16 [32, 1024, 512], P('dom', 'grp')
Inputs may be any that keep to these rules, and one draw needn't show every extreme that they name: Among the 6 slots of one subdomain at most 2 have the same owner, and in some subdomain exactly 2 do.
All inputs are finite; a program needn't handle non-finite values. No bound on the sum of `block_mask` on one device may be relied on, other than what follows from the above.
Results may differ from a plain program's by a relative error of at most 0.015.
Values may be sent and summed in bfloat16 or wider, within the bound.
A program may use at most 128 MiB of HBM per device.

v0:
```python
import jax
import jax.numpy as jnp
from jax import lax
from jax.sharding import PartitionSpec as P

BLK = 1024
COLS = 512
SLOTS = 6
OWN = 4
CAP = 2


def on_device(solved, e_blocks, block_mask, owner, local_id):
    present = block_mask[0].astype(jnp.float32)
    block_rows = BLK // lax.axis_size("grp")
    coupling = e_blocks[0, :, 0:BLK, :]
    factor = solved[0, 0:BLK, :]
    product = jnp.einsum("sjk,jc->ksc", coupling, factor, preferred_element_type=jnp.float32)
    total = product * present[:, 0][None, :, None]
    rounded = lax.optimization_barrier(total.reshape(BLK, SLOTS * COLS).astype(jnp.bfloat16))
    summed = lax.psum_scatter(
        rounded.astype(jnp.float32).astype(jnp.bfloat16), "grp", scatter_dimension=0, tiled=True
    )
    pieces = summed.reshape(block_rows, SLOTS, COLS)
    owned_ids = jnp.arange(OWN, dtype=jnp.int32)
    domains = lax.axis_size("dom")
    targets = owner[0, :, 0]
    slot_ids = jnp.arange(SLOTS, dtype=jnp.int32)
    earlier = (targets[:, None] == targets[None, :]) & (slot_ids[None, :] < slot_ids[:, None])
    position = jnp.sum(earlier.astype(jnp.int32), axis=1)
    domain_ids = jnp.arange(domains, dtype=jnp.int32)
    capacity_ids = jnp.arange(CAP, dtype=jnp.int32)
    placing = (targets[None, None, :] == domain_ids[:, None, None]) & (
        position[None, None, :] == capacity_ids[None, :, None]
    )
    placing = placing.reshape(domains * CAP, SLOTS)
    outgoing = jnp.einsum(
        "rsc,ts->rtc", pieces, placing.astype(jnp.bfloat16), preferred_element_type=jnp.float32
    ).astype(jnp.bfloat16)
    labels = jnp.sum(placing.astype(jnp.int32) * (local_id[0] + 1)[None, :], axis=1)[None, :]
    incoming, arrived = (
        lax.all_to_all(outgoing, "dom", split_axis=1, concat_axis=1, tiled=True),
        lax.all_to_all(labels, "dom", split_axis=1, concat_axis=1, tiled=True),
    )
    select = arrived[0][:, None] - 1 == owned_ids[None, :]
    result = jnp.einsum(
        "rtc,to->orc", incoming, select.astype(jnp.bfloat16), preferred_element_type=jnp.float32
    )
    return result.astype(jnp.bfloat16)


def solution(mesh):
    in_specs = (
        P("dom", "grp", None),
        P("dom", None, "grp", None),
        P("dom", None, "grp"),
        P("dom", None, None),
        P("dom", None),
    )
    out_specs = P("dom", "grp", None)
    return jax.shard_map(
        on_device, mesh=mesh, in_specs=in_specs, out_specs=out_specs, check_vma=False
    )
```

profile of v0, /device:TPU:0, one launch (start us, length us, event | category | flops | bytes accessed | tf_op | source)
XLA Modules:
  0.0 210.0 jit_solution(965573409656240507)
XLA Ops:
  6.5 0.0 copy-start
  6.5 0.0 reduce-scatter.2.cloned.1.call-start
  6.5 0.7 convert_bitcast_fusion.1
  7.3 0.5 copy-done
  7.8 13.3 %multiply_convert_fusion = bf16[512,6,1024]{2,0,1:T(8,128)(2,1)} fusion(f32[6]{0:T(128)S(1)} %convert_bitcast_fusion.1, bf16[1,6,1024,1024]{3,2,1,0:T(8,128)(2,1)} %param.6, bf16[1,1024,512]{2,1,0:T(8,128)(2,1)S(1)} %copy-done), kind=kOutput, calls=%fused_computation.2 | convolution fusion | flops 6448742400 | bytes 19922968 | tf_op jit(solution)/shard_map/sjk,jc->ksc/dot_general | solution.py:18
  21.0 0.0 copy-start.2
  21.0 0.0 copy-start.1
  21.0 0.0 reduce-scatter.2.cloned.1.call-update
  21.1 0.6 copy-done.2
  21.7 0.2 convert_reduce_fusion
  21.9 0.0 copy-done.1
  21.9 0.8 select_reduce_fusion
  22.7 5.2 %all-to-all-start = ((s32[1,8,2]{2,0,1:T(1,128)}), s32[1,8,2]{2,0,1:T(1,128)S(1)}, u32[]{:S(2)}, u32[]{:S(2)}) async-start(s32[1,8,2]{2,0,1:T(1,128)} %bitcast.13), calls=%async_computation | async-start | bytes 8192 | tf_op jit(solution)/shard_map/all_to_all | solution.py:43
  27.9 106.8 %reduce-scatter.2.cloned.1.call-done = bf16[256,3072]{0,1:T(8,128)(2,1)} async-done(((bf16[1024,3072]{0,1:T(8,128)(2,1)}), bf16[256,3072]{0,1:T(8,128)(2,1)}) %reduce-scatter.2.cloned.1.call-update) | async-done | bytes 1572880 | tf_op jit(solution)/shard_map/reduce_scatter | solution.py:21
  134.7 3.2 %copy.32 = bf16[256,6,512]{2,1,0:T(8,128)(2,1)S(1)} copy(bf16[256,6,512]{0,2,1:T(8,128)(2,1)} %bitcast.32) | data formatting | bytes 3145728 | tf_op jit(solution)/shard_map/reshape | solution.py:24
  138.0 1.2 convert_bitcast_fusion
  139.2 4.4 %copy.33 = bf16[256,16,512]{2,0,1:T(8,128)(2,1)} copy(bf16[256,16,512]{2,1,0:T(8,128)(2,1)S(1)} %convert_bitcast_fusion) | data formatting | bytes 8388608 | tf_op jit(solution)/shard_map/convert_element_type | solution.py:39
  143.6 0.0 all-to-all-done
  143.6 4.5 %all-to-all-start.1 = ((bf16[256,16,512]{2,0,1:T(8,128)(2,1)}), bf16[256,16,512]{2,0,1:T(8,128)(2,1)}, u32[]{:S(2)}, u32[]{:S(2)}) async-start(bf16[256,16,512]{2,0,1:T(8,128)(2,1)} %copy.33), calls=%async_computation.2 | async-start | bytes 8388608 | tf_op jit(solution)/shard_map/all_to_all | solution.py:42
  148.2 0.1 sub.6
  148.2 49.0 %all-to-all-done.1 = bf16[256,16,512]{2,0,1:T(8,128)(2,1)} async-done(((bf16[256,16,512]{2,0,1:T(8,128)(2,1)}), bf16[256,16,512]{2,0,1:T(8,128)(2,1)}, u32[]{:S(2)}, u32[]{:S(2)}) %all-to-all-start.1) | async-done | bytes 4194336 | tf_op jit(solution)/shard_map/all_to_all | solution.py:42
  197.2 4.7 %fusion.6 = bf16[4,256,512]{2,0,1:T(4,128)(2,1)S(1)} fusion(bf16[256,16,512]{2,0,1:T(8,128)(2,1)} %all-to-all-done.1, s32[16]{0:T(128)S(1)} %sub.6), kind=kOutput, calls=%fused_computation.6 | convolution fusion | flops 17301568 | bytes 5242944 | tf_op jit(solution)/shard_map/rtc,to->orc/dot_general | solution.py:46
  202.0 1.2 copy.35
  (5 shorter events, 0.1 us)
Async XLA Ops:
  6.5 1.2 copy-start
  6.5 128.2 %reduce-scatter.2.cloned.1.call-start = ((), (), s32[]{:S(2)}) async-start(), calls=%async_computation.3 | async-start | bytes 7864320 | tf_op jit(solution)/shard_map/reduce_scatter | solution.py:21
  21.0 0.7 copy-start.2
  21.0 0.8 copy-start.1
  22.7 120.9 %all-to-all-start = ((s32[1,8,2]{2,0,1:T(1,128)}), s32[1,8,2]{2,0,1:T(1,128)S(1)}, u32[]{:S(2)}, u32[]{:S(2)}) async-start(s32[1,8,2]{2,0,1:T(1,128)} %bitcast.13), calls=%async_computation | async-start | bytes 8192 | tf_op jit(solution)/shard_map/all_to_all | solution.py:43
  143.6 53.6 %all-to-all-start.1 = ((bf16[256,16,512]{2,0,1:T(8,128)(2,1)}), bf16[256,16,512]{2,0,1:T(8,128)(2,1)}, u32[]{:S(2)}, u32[]{:S(2)}) async-start(bf16[256,16,512]{2,0,1:T(8,128)(2,1)} %copy.33), calls=%async_computation.2 | async-start | bytes 8388608 | tf_op jit(solution)/shard_map/all_to_all | solution.py:42
Sparse Core Ops, SparseCore 0:
  21.2 113.5 reduce-scatter.1
where the time goes:
time: 210 us
  waiting for transfers between devices  156 us (74%)
  matrix products  19.2 us (9%)
  between operations  13.4 us (6%)
  local copies, waits for them, and re-layouts  10 us (5%)
  starting transfers between devices  9.74 us (5%)
    reduce_scatter x1, waiting for transfers between devices, on_device(): lax.psum_scatter(rounded.astype(jnp.float32).astype(jnp.bfloat16), 'grp',...  107 us
    all_to_all x1, waiting for transfers between devices, on_device(): lax.all_to_all(outgoing, 'dom', split_axis=1, concat_axis=1, tiled=True)  49 us
    dot_general x1, matrix products, on_device(): jnp.einsum('sjk,jc->ksc', coupling, factor, preferred_element_type=jnp.fl...  13.3 us
    all_to_all x1, starting transfers between devices, on_device(): lax.all_to_all(labels, 'dom', split_axis=1, concat_axis=1, tiled=True)  5.2 us
    dot_general x1, matrix products, on_device(): jnp.einsum('rtc,to->orc', incoming, select.astype(jnp.bfloat16), preferre...  4.73 us
    all_to_all x1, starting transfers between devices, on_device(): lax.all_to_all(outgoing, 'dom', split_axis=1, concat_axis=1, tiled=True)  4.54 us
    convert_element_type x1, local copies, waits for them, and re-layouts, on_device(): outgoing = jnp.einsum('rsc,ts->rtc', pieces, placing.astype(jnp.bfloat16)...  4.37 us
  transfers between devices with their start and end apart: 3, of which 2 were waited for; matrix products, arithmetic and copies ran while one was open for 5% of the time, Pallas kernels for 0%

commit v1 on v0

v1 whole, which is shorter than its diff:
```python
import functools

import jax
import jax.numpy as jnp
from jax import lax
from jax.experimental import pallas as pl
from jax.experimental.pallas import tpu as pltpu
from jax.sharding import PartitionSpec as P

OWN = 4
CAP = 2
LANES = 128


def kernel(
    n, n_dom, mask_ref, owner_ref, local_ref, solved_ref, e_ref, out_ref,
    factor_t, coupling, own, from_left, from_right, fin, outbox, inbox, label_out, label_in, total,
    e_sem, right_send, right_recv, left_send, left_recv, dom_send, dom_recv, label_send, label_recv,
):
    g = lax.axis_index("grp")
    me = lax.axis_index("dom")
    pieces, _, slots, width, rows = own.shape
    cols = factor_t.shape[0]

    fetches = [pltpu.make_async_copy(e_ref.at[s], coupling.at[s], e_sem.at[s]) for s in range(slots)]
    for fetch in fetches:
        fetch.start()

    barrier = pltpu.get_barrier_semaphore()

    @pl.when(g > 0)
    def _():
        pl.semaphore_signal(barrier, inc=1, device_id={"grp": g - 1})

    @pl.when(g < n - 1)
    def _():
        pl.semaphore_signal(barrier, inc=1, device_id={"grp": g + 1})

    def greet(off, carry):
        pl.semaphore_signal(barrier, inc=1, device_id={"dom": lax.rem(me + off, n_dom)})
        return carry

    lax.fori_loop(1, n_dom, greet, 0)

    for p in range(pieces):
        factor_t[p * width:(p + 1) * width, :] = solved_ref[:, p * width:(p + 1) * width].T

    def multiply(s, carry):
        pltpu.make_async_copy(e_ref.at[s], coupling.at[s], e_sem.at[s]).wait()
        present = mask_ref[s].astype(jnp.float32)
        for ch in range(n):
            product = jnp.dot(
                factor_t[...], coupling[s, :, ch * rows:(ch + 1) * rows], preferred_element_type=jnp.float32
            )
            own[:, ch, s] = (product * present).astype(jnp.bfloat16).reshape(pieces, width, rows)
        return carry

    lax.fori_loop(0, slots, multiply, 0)

    def place(d, j):
        index, label = jnp.int32(0), jnp.int32(0)
        for s in range(slots):
            position = jnp.int32(0)
            for t in range(s):
                position = position + jnp.where(owner_ref[t] == owner_ref[s], 1, 0)
            hit = jnp.where((owner_ref[s] == d) & (position == j), 1, 0)
            index = index + hit * s
            label = label + hit * (local_ref[s] + 1)
        return index, label

    def label_copy(d, source):
        return pltpu.make_async_remote_copy(
            src_ref=label_out.at[d], dst_ref=label_in.at[source],
            send_sem=label_send.at[d], recv_sem=label_recv.at[source], device_id={"dom": d},
        )

    def dom_copy(p, d, source):
        return pltpu.make_async_remote_copy(
            src_ref=outbox.at[p, d], dst_ref=inbox.at[p, source],
            send_sem=dom_send.at[p, d], recv_sem=dom_recv.at[p, source], device_id={"dom": d},
        )

    def right_copy(p, ch, source):
        return pltpu.make_async_remote_copy(
            src_ref=source.at[p, ch], dst_ref=from_left.at[p, ch],
            send_sem=right_send.at[p, ch], recv_sem=right_recv.at[p, ch], device_id={"grp": g + 1},
        )

    def left_copy(p, ch, source):
        return pltpu.make_async_remote_copy(
            src_ref=source.at[p, ch], dst_ref=from_right.at[p, ch],
            send_sem=left_send.at[p, ch], recv_sem=left_recv.at[p, ch], device_id={"grp": g - 1},
        )

    greeted = n_dom - 1 + jnp.where(g > 0, 1, 0) + jnp.where(g < n - 1, 1, 0)
    pl.semaphore_wait(barrier, greeted)

    def send_labels(off, carry):
        d = lax.rem(me + off, n_dom)
        for j in range(CAP):
            _, label = place(d, j)
            label_out[d, j] = jnp.full(label_out.shape[2:], label.astype(jnp.float32), jnp.float32)
        label_copy(d, me).start()
        return carry

    def add_to(buffer, p, ch):
        def one(s, carry):
            buffer[p, ch, s] = (
                buffer[p, ch, s].astype(jnp.float32) + own[p, ch, s].astype(jnp.float32)
            ).astype(jnp.bfloat16)
            return carry

        lax.fori_loop(0, slots, one, 0)

    def forward(p):
        def one(i, carry):
            to_right = n - 1 - i

            @pl.when((to_right > g) & (g == 0))
            def _():
                right_copy(p, to_right, own).start()

            @pl.when((i < g) & (g == n - 1))
            def _():
                left_copy(p, i, own).start()

            @pl.when((to_right > g) & (g > 0))
            def _():
                right_copy(p, to_right, from_left).wait_recv()
                add_to(from_left, p, to_right)
                right_copy(p, to_right, from_left).start()

            @pl.when((i < g) & (g < n - 1))
            def _():
                left_copy(p, i, from_right).wait_recv()
                add_to(from_right, p, i)
                left_copy(p, i, from_right).start()

            return carry

        lax.fori_loop(0, n - 1, one, 0)

    def finish(p):
        @pl.when(g > 0)
        def _():
            right_copy(p, g, from_left).wait_recv()
            add_to(from_left, p, g)

        @pl.when(g == 0)
        def _():
            left_copy(p, g, from_right).wait_recv()
            add_to(from_right, p, g)

            def one(s, carry):
                fin[s] = from_right[p, g, s]
                return carry

            lax.fori_loop(0, slots, one, 0)

        @pl.when(g == n - 1)
        def _():
            def one(s, carry):
                fin[s] = from_left[p, g, s]
                return carry

            lax.fori_loop(0, slots, one, 0)

        @pl.when((g > 0) & (g < n - 1))
        def _():
            left_copy(p, g, from_right).wait_recv()

            def one(s, carry):
                fin[s] = (
                    from_left[p, g, s].astype(jnp.float32) + from_right[p, g, s].astype(jnp.float32)
                ).astype(jnp.bfloat16)
                return carry

            lax.fori_loop(0, slots, one, 0)

        def one_domain(off, carry):
            d = lax.rem(me + off, n_dom)
            for j in range(CAP):
                index, _ = place(d, j)
                outbox[p, d, j] = fin[index]
            dom_copy(p, d, me).start()
            return carry

        lax.fori_loop(1, n_dom, one_domain, 0)
        for j in range(CAP):
            index, _ = place(me, j)
            inbox[p, me, j] = fin[index]

    tile = 32

    def merge(p):
        def arrive(off, carry):
            source = lax.rem(me + off, n_dom)
            dom_copy(p, source, source).wait_recv()
            return carry

        lax.fori_loop(1, n_dom, arrive, 0)

        def one(t, carry):
            at = pl.ds(pl.multiple_of(t * tile, tile), tile)
            sums = [jnp.zeros((tile, rows), jnp.float32) for _ in range(OWN)]
            for source in range(n_dom):
                for j in range(CAP):
                    block = inbox[p, source, j, at, :].astype(jnp.float32)
                    label = label_in[source, j, 0:1, :]
                    for o in range(OWN):
                        sums[o] = sums[o] + block * jnp.where(label == o + 1, 1.0, 0.0)
            for o in range(OWN):
                total[o, at, :] = sums[o]
            return carry

        lax.fori_loop(0, width // tile, one, 0)
        for o in range(OWN):
            out_ref[o, :, p * width:(p + 1) * width] = total[o].T.astype(jnp.bfloat16)

    forward(0)
    lax.fori_loop(1, n_dom, send_labels, 0)
    for j in range(CAP):
        _, label = place(me, j)
        label_in[me, j] = jnp.full(label_out.shape[2:], label.astype(jnp.float32), jnp.float32)
    for p in range(pieces):
        if p + 1 < pieces:
            forward(p + 1)
        finish(p)
        if p == 0:
            def labelled(off, carry):
                source = lax.rem(me + off, n_dom)
                label_copy(source, source).wait_recv()
                return carry

            lax.fori_loop(1, n_dom, labelled, 0)
        else:
            merge(p - 1)
    merge(pieces - 1)

    def drain_dom(off, carry):
        d = lax.rem(me + off, n_dom)
        label_copy(d, me).wait_send()
        for p in range(pieces):
            dom_copy(p, d, me).wait_send()
        return carry

    lax.fori_loop(1, n_dom, drain_dom, 0)

    def drain(ch, carry):
        for p in range(pieces):
            @pl.when(ch > g)
            def _():
                right_copy(p, ch, from_left).wait_send()

            @pl.when(ch < g)
            def _():
                left_copy(p, ch, from_right).wait_send()

        return carry

    lax.fori_loop(0, n, drain, 0)


def on_device(solved, e_blocks, block_mask, owner, local_id):
    n, n_dom = lax.axis_size("grp"), lax.axis_size("dom")
    _, depth, cols = solved.shape
    slots, blk = e_blocks.shape[1], e_blocks.shape[3]
    rows, width = blk // n, LANES
    pieces = cols // width
    bf16, f32 = jnp.bfloat16, jnp.float32
    smem = pl.BlockSpec(memory_space=pltpu.SMEM)
    dma = pltpu.SemaphoreType.DMA
    return pl.pallas_call(
        functools.partial(kernel, n, n_dom),
        out_shape=jax.ShapeDtypeStruct((OWN, rows, cols), bf16),
        in_specs=[smem, smem, smem, pl.BlockSpec(memory_space=pltpu.VMEM), pl.BlockSpec(memory_space=pl.ANY)],
        out_specs=pl.BlockSpec(memory_space=pltpu.VMEM),
        scratch_shapes=[
            pltpu.VMEM((cols, depth), bf16),
            pltpu.VMEM((slots, depth, blk), bf16),
            pltpu.VMEM((pieces, n, slots, width, rows), bf16),
            pltpu.VMEM((pieces, n, slots, width, rows), bf16),
            pltpu.VMEM((pieces, n, slots, width, rows), bf16),
            pltpu.VMEM((slots, width, rows), bf16),
            pltpu.VMEM((pieces, n_dom, CAP, width, rows), bf16),
            pltpu.VMEM((pieces, n_dom, CAP, width, rows), bf16),
            pltpu.VMEM((n_dom, CAP, 8, rows), f32),
            pltpu.VMEM((n_dom, CAP, 8, rows), f32),
            pltpu.VMEM((OWN, width, rows), f32),
            dma((slots,)),
            dma((pieces, n)),
            dma((pieces, n)),
            dma((pieces, n)),
            dma((pieces, n)),
            dma((pieces, n_dom)),
            dma((pieces, n_dom)),
            dma((n_dom,)),
            dma((n_dom,)),
        ],
        compiler_params=pltpu.CompilerParams(
            collective_id=0, has_side_effects=True, vmem_limit_bytes=62 * 1024 * 1024
        ),
    )(block_mask.reshape(slots), owner.reshape(slots), local_id.reshape(slots), solved[0], e_blocks[0])


def solution(mesh):
    in_specs = (
        P("dom", "grp", None),
        P("dom", None, "grp", None),
        P("dom", None, "grp"),
        P("dom", None, None),
        P("dom", None),
    )
    out_specs = P("dom", "grp", None)
    return jax.shard_map(
        on_device, mesh=mesh, in_specs=in_specs, out_specs=out_specs, check_vma=False
    )
```

time: 210 us -> 145 us (0.69); the launches traced: 210 us -> 143 us
  waiting for transfers between devices: 156 us -> 0 us
  Pallas kernels: 0 us -> 140 us
  matrix products: 19.2 us -> 0 us
  between operations: 13.4 us -> 0.01 us
  starting transfers between devices: 9.74 us -> 0 us
  local copies, waits for them, and re-layouts: 10 us -> 2.26 us
    pallas_call x0 -> x1, Pallas kernels: none -> 140 us  [on_device(): pl.pallas_call(functools.partial(kernel, n, n_dom), out_shape=jax.ShapeDt...]
    reduce_scatter x1 -> x0, waiting for transfers between devices: 107 us -> none  [on_device(): lax.psum_scatter(rounded.astype(jnp.float32).astype(jnp.bfloat16), 'grp',...]
    all_to_all x2 -> x0, waiting for transfers between devices: 49 us -> none  [the longest x1 49 us: on_device(): lax.all_to_all(outgoing, 'dom', split_axis=1, concat_axis=1, tiled=True)]
    dot_general x3 -> x0, matrix products: 19.2 us -> none  [the longest x1 13.3 us: on_device(): jnp.einsum('sjk,jc->ksc', coupling, factor, preferred_element_type=jnp.fl...]
    all_to_all x2 -> x0, starting transfers between devices: 9.74 us -> none  [the longest x1 5.2 us: on_device(): lax.all_to_all(labels, 'dom', split_axis=1, concat_axis=1, tiled=True)]
    convert_element_type x2 -> x0, local copies, waits for them, and re-layouts: 5.53 us -> none  [the longest x1 4.37 us: on_device(): outgoing = jnp.einsum('rsc,ts->rtc', pieces, placing.astype(jnp.bfloat16)...]
    reshape x1 -> x0, local copies, waits for them, and re-layouts: 3.25 us -> none  [on_device(): pieces = summed.reshape(block_rows, SLOTS, COLS)]
  transfers between devices with their start and end apart: 3 -> 0, of which waited for: 2 -> 0; matrix products, arithmetic and copies ran while one was open for 5% -> 0% of each run, Pallas kernels for 0% -> 0%
where the time goes in v1:
time: 145 us; the launch traced here: 143 us
  Pallas kernels  140 us (97%)
  local copies, waits for them, and re-layouts  2.26 us (2%)
    pallas_call x1, Pallas kernels, on_device(): pl.pallas_call(functools.partial(kernel, n, n_dom), out_shape=jax.ShapeDt...  140 us

profile of v1, /device:TPU:0, one launch (start us, length us, event | category | flops | bytes accessed | tf_op | source)
XLA Modules:
  0.0 142.6 jit_solution(8754200323293899006)
XLA Ops:
  0.0 140.3 %shard_map.55 = bf16[4,256,512]{2,1,0:T(8,128)(2,1)} custom-call(s32[6]{0:T(128)} %bitcast.7, s32[6]{0:T(128)} %bitcast.8, s32[6]{0:T(128)} %bitcast.9, bf16[1024,512]{1,0:T(8,128)(2,1)} %bitcast.6, bf16[6,1024,1024]{2,1,0:T(8,128)(2,1)} %bitcast.5), custom_call_target="tpu_custom_call" | custom-call | tf_op jit(solution)/shard_map/pallas_call | solution.py:273
  140.3 2.3 %copy.7 = bf16[4,256,512]{2,1,0:T(8,128)(2,1)} copy(bf16[4,256,512]{2,1,0:T(8,128)(2,1)} %shard_map.55) | data formatting | bytes 2097152

commit v2 on v1

--- a/solution.py
+++ b/solution.py
@@ -10,6 +10,8 @@
 OWN = 4
 CAP = 2
 LANES = 128
+SPLIT = 2
+AHEAD = 3
 
 
 def kernel(
@@ -42,20 +44,26 @@
 
     lax.fori_loop(1, n_dom, greet, 0)
 
-    for p in range(pieces):
-        factor_t[p * width:(p + 1) * width, :] = solved_ref[:, p * width:(p + 1) * width].T
-
-    def multiply(s, carry):
-        pltpu.make_async_copy(e_ref.at[s], coupling.at[s], e_sem.at[s]).wait()
-        present = mask_ref[s].astype(jnp.float32)
-        for ch in range(n):
-            product = jnp.dot(
-                factor_t[...], coupling[s, :, ch * rows:(ch + 1) * rows], preferred_element_type=jnp.float32
-            )
-            own[:, ch, s] = (product * present).astype(jnp.bfloat16).reshape(pieces, width, rows)
-        return carry
-
-    lax.fori_loop(0, slots, multiply, 0)
+    for p in range(cols // LANES):
+        factor_t[p * LANES:(p + 1) * LANES, :] = solved_ref[:, p * LANES:(p + 1) * LANES].T
+
+    def multiply(low, high, fetched):
+        def one(s, carry):
+            if not fetched:
+                pltpu.make_async_copy(e_ref.at[s], coupling.at[s], e_sem.at[s]).wait()
+            present = mask_ref[s].astype(jnp.float32)
+            for ch in range(n):
+                product = jnp.dot(
+                    factor_t[low * width:high * width, :],
+                    coupling[s, :, ch * rows:(ch + 1) * rows],
+                    preferred_element_type=jnp.float32,
+                )
+                own[low:high, ch, s] = (product * present).astype(jnp.bfloat16).reshape(high - low, width, rows)
+            return carry
+
+        lax.fori_loop(0, slots, one, 0)
+
+    multiply(0, SPLIT, False)
 
     def place(d, j):
         index, label = jnp.int32(0), jnp.int32(0)
@@ -112,17 +120,25 @@
 
         lax.fori_loop(0, slots, one, 0)
 
+    def start_ends(p):
+        def one(i, carry):
+            to_right = n - 1 - i
+
+            @pl.when((to_right > g) & (g == 0))
+            def _():
+                right_copy(p, to_right, own).start()
+
+            @pl.when((i < g) & (g == n - 1))
+            def _():
+                left_copy(p, i, own).start()
+
+            return carry
+
+        lax.fori_loop(0, n - 1, one, 0)
+
     def forward(p):
         def one(i, carry):
             to_right = n - 1 - i
-
-            @pl.when((to_right > g) & (g == 0))
-            def _():
-                right_copy(p, to_right, own).start()
-
-            @pl.when((i < g) & (g == n - 1))
-            def _():
-                left_copy(p, i, own).start()
 
             @pl.when((to_right > g) & (g > 0))
             def _():
@@ -200,8 +216,11 @@
 
         lax.fori_loop(1, n_dom, arrive, 0)
 
+        half = lax.rem(p, SPLIT) * width
+
         def one(t, carry):
             at = pl.ds(pl.multiple_of(t * tile, tile), tile)
+            put = pl.ds(pl.multiple_of(half + t * tile, tile), tile)
             sums = [jnp.zeros((tile, rows), jnp.float32) for _ in range(OWN)]
             for source in range(n_dom):
                 for j in range(CAP):
@@ -210,32 +229,50 @@
                     for o in range(OWN):
                         sums[o] = sums[o] + block * jnp.where(label == o + 1, 1.0, 0.0)
             for o in range(OWN):
-                total[o, at, :] = sums[o]
+                total[o, put, :] = sums[o]
             return carry
 
         lax.fori_loop(0, width // tile, one, 0)
-        for o in range(OWN):
-            out_ref[o, :, p * width:(p + 1) * width] = total[o].T.astype(jnp.bfloat16)
-
-    forward(0)
+        @pl.when(lax.rem(p, SPLIT) == SPLIT - 1)
+        def _():
+            lanes = pl.ds(pl.multiple_of((p // SPLIT) * LANES, LANES), LANES)
+            for o in range(OWN):
+                out_ref[o, :, lanes] = total[o].T.astype(jnp.bfloat16)
+
+    for p in range(SPLIT):
+        start_ends(p)
+    multiply(SPLIT, pieces, True)
+    for p in range(SPLIT, AHEAD):
+        start_ends(p)
     lax.fori_loop(1, n_dom, send_labels, 0)
     for j in range(CAP):
         _, label = place(me, j)
         label_in[me, j] = jnp.full(label_out.shape[2:], label.astype(jnp.float32), jnp.float32)
-    for p in range(pieces):
-        if p + 1 < pieces:
-            forward(p + 1)
+    def step(p, carry):
+        @pl.when(p + AHEAD < pieces)
+        def _():
+            start_ends(p + AHEAD)
+
+        forward(p)
         finish(p)
-        if p == 0:
+
+        @pl.when(p == 0)
+        def _():
             def labelled(off, carry):
                 source = lax.rem(me + off, n_dom)
                 label_copy(source, source).wait_recv()
                 return carry
 
             lax.fori_loop(1, n_dom, labelled, 0)
-        else:
+
+        @pl.when(p > 0)
+        def _():
             merge(p - 1)
-    merge(pieces - 1)
+
+        return carry
+
+    lax.fori_loop(0, pieces, step, 0)
+    merge(jnp.int32(pieces - 1))
 
     def drain_dom(off, carry):
         d = lax.rem(me + off, n_dom)
@@ -265,7 +302,7 @@
     n, n_dom = lax.axis_size("grp"), lax.axis_size("dom")
     _, depth, cols = solved.shape
     slots, blk = e_blocks.shape[1], e_blocks.shape[3]
-    rows, width = blk // n, LANES
+    rows, width = blk // n, LANES // SPLIT
     pieces = cols // width
     bf16, f32 = jnp.bfloat16, jnp.float32
     smem = pl.BlockSpec(memory_space=pltpu.SMEM)
@@ -286,7 +323,7 @@
             pltpu.VMEM((pieces, n_dom, CAP, width, rows), bf16),
             pltpu.VMEM((n_dom, CAP, 8, rows), f32),
             pltpu.VMEM((n_dom, CAP, 8, rows), f32),
-            pltpu.VMEM((OWN, width, rows), f32),
+            pltpu.VMEM((OWN, LANES, rows), f32),
             dma((slots,)),
             dma((pieces, n)),
             dma((pieces, n)),

time: 145 us -> 157 us (1.083); the launches traced: 143 us -> 156 us
  Pallas kernels: 140 us -> 154 us
    pallas_call x1, Pallas kernels: 140 us -> 154 us  [on_device(): pl.pallas_call(functools.partial(kernel, n, n_dom), out_shape=jax.ShapeDt...]
where the time goes in v2:
time: 157 us; the launch traced here: 156 us
  Pallas kernels  154 us (98%)
  local copies, waits for them, and re-layouts  2.26 us (1%)
    pallas_call x1, Pallas kernels, on_device(): pl.pallas_call(functools.partial(kernel, n, n_dom), out_shape=jax.ShapeDt...  154 us

profile of v2, /device:TPU:0, one launch (start us, length us, event | category | flops | bytes accessed | tf_op | source)
XLA Modules:
  0.0 156.4 jit_solution(4238674824792194311)
XLA Ops:
  0.0 154.1 %shard_map.55 = bf16[4,256,512]{2,1,0:T(8,128)(2,1)} custom-call(s32[6]{0:T(128)} %bitcast.7, s32[6]{0:T(128)} %bitcast.8, s32[6]{0:T(128)} %bitcast.9, bf16[1024,512]{1,0:T(8,128)(2,1)} %bitcast.6, bf16[6,1024,1024]{2,1,0:T(8,128)(2,1)} %bitcast.5), custom_call_target="tpu_custom_call" | custom-call | tf_op jit(solution)/shard_map/pallas_call | solution.py:310
  154.1 2.3 %copy.7 = bf16[4,256,512]{2,1,0:T(8,128)(2,1)} copy(bf16[4,256,512]{2,1,0:T(8,128)(2,1)} %shard_map.55) | data formatting | bytes 2097152
